TPU v7x, 32 devices: a whole 2x2x4 slice. The times are simulated.
32 devices in a mesh: lon: 8 (over z, y), lat: 4 (over x, core).
Axes of the slice: x: 2, y: 2, z: 4, core: 2. Of those that a mesh axis runs over, the one named last changes fastest.
Arguments:
- terrain_relief: float32 [1, 2688, 10752], P(None, 'lon', 'lat'), may hold values from -30 to 30
Outputs:
- smoothed: float32 [1, 2688, 10752], P(None, 'lon', 'lat')
- slope: float32 [1, 2688, 10752], P(None, 'lon', 'lat')
All inputs are finite; a program needn't handle non-finite values.
Results may differ from a plain program's by a relative error of at most 0.0001.
Values sent between devices are 32-bit elements; how exact they have to be, the bound alone decides.
A program may use at most 64 MiB of HBM per device.

v0:
```python
import jax
import jax.numpy as jnp
from jax import lax
from jax.sharding import PartitionSpec as P


def with_halo(cells, sides, width, closed):
    for axis, dim in sides:
        count = lax.axis_size(axis)
        ends = count if closed else count - 1
        head = lax.slice_in_dim(cells, 0, width, axis=dim)
        tail = lax.slice_in_dim(cells, cells.shape[dim] - width, cells.shape[dim], axis=dim)
        cells = jnp.concatenate(
            [
                lax.ppermute(tail, axis, [(i, (i + 1) % count) for i in range(ends)]),
                cells,
                lax.ppermute(head, axis, [((i + 1) % count, i) for i in range(ends)]),
            ],
            axis=dim,
        )
    return cells


def extend(relief_surface, width):
    widened = with_halo(relief_surface, (("lon", 1),), width, True)
    return with_halo(widened, (("lat", 2),), width, False)


def box_mean(extended, first_row, total_rows):
    col_span = extended.shape[1] - 4
    row_span = extended.shape[2] - 4
    lon_sum = sum((extended[:, offset : offset + col_span, :] for offset in range(5)))
    box_total = sum((lon_sum[:, :, offset : offset + row_span] for offset in range(5)))
    global_rows = first_row + 2 + jnp.arange(row_span, dtype=jnp.int32)
    counted = jnp.maximum(
        jnp.minimum(global_rows + 2, total_rows - 1) - jnp.maximum(global_rows - 2, 0) + 1, 1
    ).astype(jnp.float32)
    inside = (global_rows >= 0) & (global_rows < total_rows)
    return jnp.where(inside, box_total / (5.0 * counted), 0.0)


def polar_restore(relief_surface, first_row, lead, meridian_count, total_rows, total_cols):
    global_rows = first_row + jnp.arange(relief_surface.shape[2], dtype=jnp.int32)
    north = global_rows == 0
    south = global_rows == total_rows - 1
    inner = relief_surface[:, lead : lead + meridian_count, :]
    northern_portion = jnp.sum(jnp.where(north, inner, 0.0), axis=(1, 2))
    south_part = jnp.sum(jnp.where(south, inner, 0.0), axis=(1, 2))
    totals = lax.psum((northern_portion, south_part), "lon")
    north_mean = totals[0] / total_cols
    south_mean = totals[1] / total_cols
    relief_surface = jnp.where(north, north_mean[:, None, None], relief_surface)
    return jnp.where(south, south_mean[:, None, None], relief_surface)


def horn_slope(extended, first_row, total_rows):
    across = extended[:, 2:, :] - extended[:, :-2, :]
    east_west = across[:, :, :-2] + 2.0 * across[:, :, 1:-1] + across[:, :, 2:]
    upward = extended[:, :, 2:] - extended[:, :, :-2]
    north_south = upward[:, :-2, :] + 2.0 * upward[:, 1:-1, :] + upward[:, 2:, :]
    parallel_count = east_west.shape[2]
    global_rows = (first_row + 1 + jnp.arange(parallel_count, dtype=jnp.int32)).astype(jnp.float32)
    latitude = jnp.pi * ((global_rows + 0.5) / total_rows - 0.5)
    stretch = 1.0 / jnp.maximum(jnp.cos(latitude), 0.1)
    grad_x = east_west * stretch / 8.0
    grad_y = north_south / 8.0
    return jnp.sqrt(1.0 + grad_x * grad_x + grad_y * grad_y)


def local(terrain_relief):
    meridian_count = terrain_relief.shape[1]
    parallel_count = terrain_relief.shape[2]
    total_cols = meridian_count * lax.axis_size("lon")
    total_rows = parallel_count * lax.axis_size("lat")
    band_start = lax.axis_index("lat") * parallel_count
    grown = extend(terrain_relief, 5)
    relief_surface = box_mean(grown, band_start - 5, total_rows)
    relief_surface = polar_restore(
        relief_surface, band_start - 3, 3, meridian_count, total_rows, total_cols
    )
    relief_surface = box_mean(relief_surface, band_start - 3, total_rows)
    relief_surface = polar_restore(
        relief_surface, band_start - 1, 1, meridian_count, total_rows, total_cols
    )
    smoothed = relief_surface[:, 1:-1, 1:-1]
    slope = horn_slope(relief_surface, band_start - 1, total_rows)
    return (smoothed, slope)


def solution(mesh):
    placed = (P(None, "lon", "lat"),)
    return jax.shard_map(
        local,
        mesh=mesh,
        in_specs=placed,
        out_specs=(P(None, "lon", "lat"), P(None, "lon", "lat")),
        check_vma=False,
    )
```

profile of v0, /device:TPU:2, one launch (start us, length us, event | category | flops | bytes accessed | tf_op | source)
XLA Modules:
  0.0 125.3 jit_solution(17069309590906123955)
XLA Ops:
  0.6 0.9 fusion.25
  1.6 4.6 %collective-permute-start.1 = (f32[1,5,2688]{2,1,0:T(8,128)S(1)}, f32[1,5,2688]{2,1,0:T(8,128)S(1)}, u32[]{:S(2)}, u32[]{:S(2)}) collective-permute-start(f32[1,5,2688]{2,1,0:T(8,128)S(1)} %get-tuple-element.13), channel_id=1, source_target_pairs={{4,0},{8,4},{12,8},{16,12},{20,16},{24,20},{28,24},{0,28},{5,1},{9... | collective-permute-start | bytes 161288 | tf_op jit(solution)/shard_map/ppermute | solution.py:17
  6.2 0.0 collective-permute-start
  6.3 0.1 maximum_divide_fusion
  6.4 1.9 %collective-permute-done.1 = f32[1,5,2688]{2,1,0:T(8,128)S(1)} collective-permute-done((f32[1,5,2688]{2,1,0:T(8,128)S(1)}, f32[1,5,2688]{2,1,0:T(8,128)S(1)}, u32[]{:S(2)}, u32[]{:S(2)}) %collective-permute-start.1) | collective-permute-done | bytes 53792 | tf_op jit(solution)/shard_map/ppermute | solution.py:17
  8.3 5.1 %collective-permute-done = f32[1,5,2688]{2,1,0:T(8,128)S(1)} collective-permute-done((f32[1,5,2688]{2,1,0:T(8,128)S(1)}, f32[1,5,2688]{2,1,0:T(8,128)S(1)}, u32[]{:S(2)}, u32[]{:S(2)}) %collective-permute-start) | collective-permute-done | bytes 53792 | tf_op jit(solution)/shard_map/ppermute | solution.py:15
  13.4 2.3 %pad_maximum_fusion = f32[1,346,2688]{2,1,0:T(8,128)S(1)} fusion(f32[1,5,2688]{2,1,0:T(8,128)S(1)} %collective-permute-done.1, f32[1,336,2688]{2,1,0:T(8,128)} %param.1, f32[1,5,2688]{2,1,0:T(8,128)S(1)} %collective-permute-done), kind=kLoop, calls=%fused_computation.23 | loop fusion | flops 1860096 | bytes 7440384 | tf_op jit(solution)/shard_map/concatenate | solution.py:13
  15.7 0.0 copy-start.2
  15.7 1.9 %copy-done.2 = f32[1,346,2688]{2,1,0:T(8,128)} copy-done((f32[1,346,2688]{2,1,0:T(8,128)}, f32[1,346,2688]{2,1,0:T(8,128)S(1)}, u32[]{:S(2)}) %copy-start.2) | copy-done | bytes 3720216
  17.5 0.1 fusion.24
  17.7 1.9 %collective-permute-start.2 = (f32[1,346,5]{2,1,0:T(8,128)S(1)}, f32[1,346,5]{2,1,0:T(8,128)S(1)}, u32[]{:S(2)}, u32[]{:S(2)}) collective-permute-start(f32[1,346,5]{2,1,0:T(8,128)S(1)} %get-tuple-element.11), channel_id=1, source_target_pairs={{0,1},{1,2},{2,3},{4,5},{5,6},{6,7},{8,9},{9,10},{10,11},{12,13},{... | collective-permute-start | bytes 20768 | tf_op jit(solution)/shard_map/ppermute | solution.py:15
  19.6 3.6 %collective-permute-start.3 = (f32[1,346,5]{2,1,0:T(8,128)S(1)}, f32[1,346,5]{2,1,0:T(8,128)S(1)}, u32[]{:S(2)}, u32[]{:S(2)}) collective-permute-start(f32[1,346,5]{2,1,0:T(8,128)S(1)} %get-tuple-element.10), channel_id=1, source_target_pairs={{1,0},{2,1},{3,2},{5,4},{6,5},{7,6},{9,8},{10,9},{11,10},{13,12},{... | collective-permute-start | bytes 20768 | tf_op jit(solution)/shard_map/ppermute | solution.py:17
  23.3 1.2 collective-permute-done.2
  24.5 1.8 %collective-permute-done.3 = f32[1,346,5]{2,1,0:T(8,128)S(1)} collective-permute-done((f32[1,346,5]{2,1,0:T(8,128)S(1)}, f32[1,346,5]{2,1,0:T(8,128)S(1)}, u32[]{:S(2)}, u32[]{:S(2)}) %collective-permute-start.3) | collective-permute-done | bytes 6952 | tf_op jit(solution)/shard_map/ppermute | solution.py:17
  26.2 5.2 %concatenate.7 = f32[1,346,2698]{2,1,0:T(8,128)} concatenate(f32[1,346,5]{2,1,0:T(8,128)S(1)} %collective-permute-done.2, f32[1,346,2688]{2,1,0:T(8,128)} %copy-done.2, f32[1,346,5]{2,1,0:T(8,128)S(1)} %collective-permute-done.3), dimensions={2} | concatenate | bytes 7468064 | tf_op jit(solution)/shard_map/concatenate | solution.py:13
  31.4 8.4 %slice_add_fusion.12 = f32[1,342,2698]{2,1,0:T(8,128)S(1)} fusion(f32[1,346,2698]{2,1,0:T(8,128)} %concatenate.7), kind=kLoop, calls=%fused_computation.16 | loop fusion | flops 3690864 | bytes 22145184 | tf_op jit(solution)/shard_map/add | solution.py:32
  39.8 0.0 copy-start.1
  39.8 4.3 %fusion.3 = f32[1,342,2694]{2,1,0:T(8,128)S(1)} fusion(f32[1,342,2698]{2,1,0:T(8,128)S(1)} %slice_add_fusion.12, f32[2694]{0:T(1024)S(1)} %convert_multiply_fusion.1, pred[2694]{0:T(1024)(128)(4,1)S(1)} %fusion.23), kind=kLoop, calls=%fused_computation.12 | loop fusion | flops 5528088 | bytes 22125822 | tf_op jit(solution)/shard_map/jit(_where)/select_n | solution.py:39
  44.1 0.0 copy-done.1
  44.1 1.6 %select_reduce_fusion.3 = (f32[]{:T(128)}, f32[]{:T(128)}) fusion(f32[1,342,2694]{2,1,0:T(8,128)S(1)} %fusion.3, pred[2694]{0:T(1024)(128)(4,1)S(1)} %get-tuple-element.15, pred[2694]{0:T(1024)(128)(4,1)S(1)} %get-tuple-element.14), kind=kLoop, calls=%fused_computation.27 | loop fusion | flops 3620734 | bytes 3626132 | tf_op jit(solution)/shard_map/reduce_sum | solution.py:48
  45.7 17.8 %all-reduce.1 = (f32[1]{0:T(128)}, f32[1]{0:T(128)}) all-reduce(f32[1]{0:T(128)} %bitcast.2, f32[1]{0:T(128)} %bitcast), channel_id=1, replica_groups=mesh['lon'=8,'lat'=4] {'lon'}, use_global_device_ids=true, to_apply=%region_3.4 | all-reduce | flops 2 | bytes 16 | tf_op jit(solution)/shard_map/psum | solution.py:49
  64.8 11.6 %select_select_fusion.1 = f32[1,342,2694]{2,1,0:T(8,128)S(1)} fusion(f32[]{:T(128)} %bitcast.3, f32[]{:T(128)} %bitcast.1, pred[2694]{0:T(1024)(128)(4,1)S(1)} %get-tuple-element.14, pred[2694]{0:T(1024)(128)(4,1)S(1)} %get-tuple-element.15, f32[2694]{0:T(1024)S(1)} %convert_multiply_fusion.1, f32[1,342,2698]{2,1,0:T(8,128)} %copy-done.1, ...), kind=kLoop, calls=%fused_computation.21 | loop fusion | flops 7370784 | bytes 22131218 | tf_op jit(solution)/shard_map/jit(_where)/select_n | solution.py:53
  76.4 1.6 %slice_add_fusion.4 = f32[1,338,2694]{2,1,0:T(8,128)S(1)} fusion(f32[1,342,2694]{2,1,0:T(8,128)S(1)} %select_select_fusion.1), kind=kLoop, calls=%fused_computation.6 | loop fusion | flops 3642288 | bytes 21853728 | tf_op jit(solution)/shard_map/add | solution.py:32
  77.9 0.0 copy-start
  78.0 4.3 %fusion.1 = f32[1,338,2690]{2,1,0:T(8,128)S(1)} fusion(f32[1,338,2694]{2,1,0:T(8,128)S(1)} %slice_add_fusion.4, f32[2690]{0:T(1024)S(1)} %convert_multiply_fusion, pred[2690]{0:T(1024)(128)(4,1)S(1)} %fusion.22), kind=kLoop, calls=%fused_computation.2 | loop fusion | flops 5455320 | bytes 21834730 | tf_op jit(solution)/shard_map/jit(_where)/select_n | solution.py:39
  82.2 0.0 copy-done
  82.2 1.6 %select_reduce_fusion.1 = (f32[]{:T(128)}, f32[]{:T(128)}) fusion(f32[1,338,2690]{2,1,0:T(8,128)S(1)} %fusion.1, pred[2690]{0:T(1024)(128)(4,1)S(1)} %get-tuple-element.17, pred[2690]{0:T(1024)(128)(4,1)S(1)} %get-tuple-element.16), kind=kLoop, calls=%fused_computation.25 | loop fusion | flops 3615358 | bytes 3620748 | tf_op jit(solution)/shard_map/reduce_sum | solution.py:48
  83.9 19.9 %all-reduce = (f32[1]{0:T(128)}, f32[1]{0:T(128)}) all-reduce(f32[1]{0:T(128)} %bitcast.6, f32[1]{0:T(128)} %bitcast.4), channel_id=1, replica_groups=mesh['lon'=8,'lat'=4] {'lon'}, use_global_device_ids=true, to_apply=%region_7.8 | all-reduce | flops 2 | bytes 16 | tf_op jit(solution)/shard_map/psum | solution.py:49
  105.1 11.6 %select_select_fusion = f32[1,338,2690]{2,1,0:T(8,128)S(1)} fusion(f32[]{:T(128)} %bitcast.7, f32[]{:T(128)} %bitcast.5, pred[2690]{0:T(1024)(128)(4,1)S(1)} %get-tuple-element.16, pred[2690]{0:T(1024)(128)(4,1)S(1)} %get-tuple-element.17, f32[2690]{0:T(1024)S(1)} %convert_multiply_fusion, f32[1,338,2694]{2,1,0:T(8,128)} %copy-done, ...), kind=kLoop, calls=%fused_computation.20 | loop fusion | flops 7273760 | bytes 21840118 | tf_op jit(solution)/shard_map/jit(_where)/select_n | solution.py:53
  116.7 2.8 %slice.172 = f32[1,336,2688]{2,1,0:T(8,128)} slice(f32[1,338,2690]{2,1,0:T(8,128)S(1)} %select_select_fusion), slice={[0:1], [1:337], [1:2689]} | slice | bytes 7225344 | tf_op jit(solution)/shard_map/slice | solution.py:85
  119.5 1.0 slice_subtract_fusion.1
  120.5 0.4 slice_subtract_fusion
  120.9 4.4 %fusion.7 = f32[1,336,2688]{2,1,0:T(8,128)} fusion(f32[1,338,2688]{2,1,0:T(8,128)S(1)} %slice_subtract_fusion.1, f32[1,336,2690]{2,1,0:T(8,128)S(1)} %slice_subtract_fusion, f32[2688]{0:T(1024)S(1)} %maximum_divide_fusion), kind=kLoop, calls=%fused_computation.33 | loop fusion | flops 11741184 | bytes 25299456 | tf_op jit(solution)/shard_map/sqrt | solution.py:67
  (6 shorter events, 0.1 us)
Async XLA Ops:
  1.6 6.7 %collective-permute-start.1 = (f32[1,5,2688]{2,1,0:T(8,128)S(1)}, f32[1,5,2688]{2,1,0:T(8,128)S(1)}, u32[]{:S(2)}, u32[]{:S(2)}) collective-permute-start(f32[1,5,2688]{2,1,0:T(8,128)S(1)} %get-tuple-element.13), channel_id=1, source_target_pairs={{4,0},{8,4},{12,8},{16,12},{20,16},{24,20},{28,24},{0,28},{5,1},{9... | collective-permute-start | bytes 161288 | tf_op jit(solution)/shard_map/ppermute | solution.py:17
  6.2 7.2 %collective-permute-start = (f32[1,5,2688]{2,1,0:T(8,128)S(1)}, f32[1,5,2688]{2,1,0:T(8,128)S(1)}, u32[]{:S(2)}, u32[]{:S(2)}) collective-permute-start(f32[1,5,2688]{2,1,0:T(8,128)S(1)} %get-tuple-element.12), channel_id=1, source_target_pairs={{0,4},{4,8},{8,12},{12,16},{16,20},{20,24},{24,28},{28,0},{1,5},{5... | collective-permute-start | bytes 161288 | tf_op jit(solution)/shard_map/ppermute | solution.py:15
  15.7 1.9 %copy-start.2 = (f32[1,346,2688]{2,1,0:T(8,128)}, f32[1,346,2688]{2,1,0:T(8,128)S(1)}, u32[]{:S(2)}) copy-start(f32[1,346,2688]{2,1,0:T(8,128)S(1)} %pad_maximum_fusion) | copy-start | bytes 11160580
  17.7 6.8 %collective-permute-start.2 = (f32[1,346,5]{2,1,0:T(8,128)S(1)}, f32[1,346,5]{2,1,0:T(8,128)S(1)}, u32[]{:S(2)}, u32[]{:S(2)}) collective-permute-start(f32[1,346,5]{2,1,0:T(8,128)S(1)} %get-tuple-element.11), channel_id=1, source_target_pairs={{0,1},{1,2},{2,3},{4,5},{5,6},{6,7},{8,9},{9,10},{10,11},{12,13},{... | collective-permute-start | bytes 20768 | tf_op jit(solution)/shard_map/ppermute | solution.py:15
  19.6 6.6 %collective-permute-start.3 = (f32[1,346,5]{2,1,0:T(8,128)S(1)}, f32[1,346,5]{2,1,0:T(8,128)S(1)}, u32[]{:S(2)}, u32[]{:S(2)}) collective-permute-start(f32[1,346,5]{2,1,0:T(8,128)S(1)} %get-tuple-element.10), channel_id=1, source_target_pairs={{1,0},{2,1},{3,2},{5,4},{6,5},{7,6},{9,8},{10,9},{11,10},{13,12},{... | collective-permute-start | bytes 20768 | tf_op jit(solution)/shard_map/ppermute | solution.py:17
  39.8 4.3 %copy-start.1 = (f32[1,342,2698]{2,1,0:T(8,128)}, f32[1,342,2698]{2,1,0:T(8,128)S(1)}, u32[]{:S(2)}) copy-start(f32[1,342,2698]{2,1,0:T(8,128)S(1)} %slice_add_fusion.12) | copy-start | bytes 11072596
  77.9 4.3 %copy-start = (f32[1,338,2694]{2,1,0:T(8,128)}, f32[1,338,2694]{2,1,0:T(8,128)S(1)}, u32[]{:S(2)}) copy-start(f32[1,338,2694]{2,1,0:T(8,128)S(1)} %slice_add_fusion.4) | copy-start | bytes 10926868
where the time goes:
time: 126 us; the launch traced here: 125 us
  other arithmetic  53.2 us (42%)
  blocking collectives  37.7 us (30%)
  local copies, waits for them, and re-layouts  10.9 us (9%)
  starting transfers between devices  10.2 us (8%)
  waiting for transfers between devices  9.99 us (8%)
  between operations  3.41 us (3%)
    psum x2, blocking collectives, polar_restore(): totals = lax.psum((northern_portion, south_part), 'lon')  37.7 us
    select_n x2, other arithmetic, polar_restore(): return jnp.where(south, south_mean[:, None, None], relief_surface)  23.2 us
    add x2, other arithmetic, box_mean(): sum((extended[:, offset:offset + col_span, :] for offset in range(5)))  9.96 us
    select_n x2, other arithmetic, box_mean(): return jnp.where(inside, box_total / (5.0 * counted), 0.0)  8.53 us
    ppermute x2, starting transfers between devices, with_halo(): lax.ppermute(head, axis, [((i + 1) % count, i) for i in range(ends)])  8.25 us
    ppermute x2, waiting for transfers between devices, with_halo(): lax.ppermute(tail, axis, [(i, (i + 1) % count) for i in range(ends)])  6.3 us
    concatenate x1, local copies, waits for them, and re-layouts, with_halo(): jnp.concatenate([lax.ppermute(tail, axis, [(i, (i + 1) % count) for i in...  5.15 us
    sqrt x1, other arithmetic, horn_slope(): return jnp.sqrt(1.0 + grad_x * grad_x + grad_y * grad_y)  4.38 us
  transfers between devices with their start and end apart: 4, of which 4 were waited for; matrix products, arithmetic and copies ran while one was open for 0% of the time, Pallas kernels for 0%

commit v1 on v0

v1 whole, which is shorter than its diff:
```python
import functools

import jax
import jax.numpy as jnp
from jax import lax
from jax.experimental import pallas as pl
from jax.experimental.pallas import tpu as pltpu
from jax.sharding import PartitionSpec as P

LANES = 128
SUB = 8
PAD = 16


class Strip:
    def __init__(self, count, make):
        self.count, self.make = count, make
        self.values, self.rolled = {}, {}

    def __getitem__(self, block):
        block %= self.count
        if block not in self.values:
            self.values[block] = self.make(block)
        return self.values[block]

    def roll(self, block, shift):
        key = (block % self.count, shift)
        if key not in self.rolled:
            self.rolled[key] = pltpu.roll(self[block], (-shift) % LANES, 1)
        return self.rolled[key]

    def ahead(self, block, shift, lane):
        if shift > 0:
            return jnp.where(lane < LANES - shift, self.roll(block, shift), self.roll(block + 1, shift))
        return jnp.where(lane >= -shift, self.roll(block, shift), self.roll(block - 1, shift))


def box_strip(src, dst, row, blocks, total_blocks, lane, scale, extra):
    def lon_sum(b):
        rows = [src[b, pl.ds(row + d, SUB), :] for d in (-2, -1, 0, 1, 2)]
        return ((rows[0] + rows[1]) + (rows[3] + rows[4])) + rows[2]

    one = Strip(total_blocks, lon_sum)
    two = Strip(total_blocks, lambda b: one[b] + one.ahead(b, 1, lane))
    for b in blocks:
        total = (two[b] + two.ahead(b, -2, lane)) + one.ahead(b, 2, lane)
        if b in scale:
            value = total * scale[b] + extra[b]
        else:
            value = total * (1.0 / 25.0)
        dst[b, pl.ds(row, SUB), :] = value
        yield b, value


def run(strip):
    for _ in strip:
        pass


def edge_rows(blocks, rows_here, start, lane):
    inner = blocks - 1
    return {
        0: start + lane,
        inner - 1: start + rows_here - LANES + lane,
        inner: jnp.where(lane < LANES // 2, start + rows_here + lane, start - LANES + lane),
    }


def edge_factors(blocks, rows_here, total_rows, start, lane, mean):
    scale, extra = {}, {}
    for b, row in edge_rows(blocks, rows_here, start, lane).items():
        low = jnp.maximum(row - 2, 0)
        high = jnp.minimum(row + 2, total_rows - 1)
        counted = jnp.maximum(high - low + 1, 1).astype(jnp.float32)
        polar = (row == 0) | (row == total_rows - 1)
        inside = (row > 0) & (row < total_rows - 1)
        scale[b] = jnp.where(inside, 1.0 / (5.0 * counted), 0.0)
        extra[b] = jnp.where(polar, mean, 0.0)
    return scale, extra


def first_kernel(n_lon, n_lat, cols, rows_here, x_hbm, z1, means, x, e, gat, in_sem, send, recv, gsend, grecv):
    inner = rows_here // LANES
    blocks = inner + 1
    lon, lat = lax.axis_index("lon"), lax.axis_index("lat")
    total_rows = rows_here * n_lat
    east, west = lax.rem(lon + 1, n_lon), lax.rem(lon + n_lon - 1, n_lon)
    has_north, has_south = lat > 0, lat < n_lat - 1
    pole = jnp.logical_not(has_north & has_south)
    lane = lax.broadcasted_iota(jnp.int32, (SUB, LANES), 1)

    loads = [
        pltpu.make_async_copy(
            x_hbm.at[0, :, pl.ds(b * LANES, LANES)], x.at[b, pl.ds(PAD, cols), :], in_sem.at[b]
        )
        for b in range(inner)
    ]
    for b in [0, inner - 1] + list(range(1, inner - 1)):
        loads[b].start()

    barrier = pltpu.get_barrier_semaphore()

    def greet(to_lon, to_lat):
        pl.semaphore_signal(
            barrier, inc=1, device_id=(to_lon, to_lat), device_id_type=pl.DeviceIdType.MESH
        )

    greet(east, lat)
    greet(west, lat)

    @pl.when(has_north)
    def _():
        for to_lon in (lon, east, west):
            greet(to_lon, lat - 1)

    @pl.when(has_south)
    def _():
        for to_lon in (lon, east, west):
            greet(to_lon, lat + 1)

    @pl.when(pole)
    def _():
        def one(d, carry):
            greet(lax.rem(lon + d, n_lon), lat)
            return carry

        lax.fori_loop(2, n_lon - 1, one, 0)

    def remote(src, dst, i, to_lon, to_lat):
        return pltpu.make_async_remote_copy(
            src_ref=src,
            dst_ref=dst,
            send_sem=send.at[i],
            recv_sem=recv.at[i],
            device_id=(to_lon, to_lat),
            device_id_type=pl.DeviceIdType.MESH,
        )

    own = pl.ds(PAD, cols)
    head, tail = pl.ds(PAD, SUB), pl.ds(PAD + cols - SUB, SUB)
    before, after = pl.ds(PAD - SUB, SUB), pl.ds(PAD + cols, SUB)
    band = pl.ds(0, inner)
    last = inner - 1
    lon_copies = [
        remote(x.at[band, tail, :], x.at[band, before, :], 0, east, lat),
        remote(x.at[band, head, :], x.at[band, after, :], 1, west, lat),
    ]
    south_copies = [
        remote(x.at[last, own, :], e.at[0, own, :], 2, lon, lat + 1),
        remote(x.at[last, tail, :], e.at[0, before, :], 3, east, lat + 1),
        remote(x.at[last, head, :], e.at[0, after, :], 4, west, lat + 1),
    ]
    north_copies = [
        remote(x.at[0, own, :], e.at[1, own, :], 5, lon, lat - 1),
        remote(x.at[0, tail, :], e.at[1, before, :], 6, east, lat - 1),
        remote(x.at[0, head, :], e.at[1, after, :], 7, west, lat - 1),
    ]

    def gather_copy(d):
        return pltpu.make_async_remote_copy(
            src_ref=gat.at[0],
            dst_ref=gat.at[d],
            send_sem=gsend.at[d],
            recv_sem=grecv.at[d],
            device_id=(lax.rem(lon + d, n_lon), lat),
            device_id_type=pl.DeviceIdType.MESH,
        )

    loads[0].wait()
    loads[last].wait()

    def partial_sum(block):
        def one(t, total):
            return total + x[block, pl.ds(pl.multiple_of(PAD + t * SUB, SUB), SUB), :]

        gat[0] = lax.fori_loop(0, cols // SUB, one, jnp.zeros((SUB, LANES), jnp.float32), unroll=True)

    pl.when(lat == 0)(lambda: partial_sum(0))
    pl.when(lat == n_lat - 1)(lambda: partial_sum(last))

    signals = 2 + 3 * has_north.astype(jnp.int32) + 3 * has_south.astype(jnp.int32)
    signals = signals + (n_lon - 3) * pole.astype(jnp.int32)
    pl.semaphore_wait(barrier, signals)

    @pl.when(has_south)
    def _():
        for copy in south_copies:
            copy.start()

    @pl.when(has_north)
    def _():
        for copy in north_copies:
            copy.start()

    for b in range(1, last):
        loads[b].wait()
    for copy in lon_copies:
        copy.start()

    def each_gather(act):
        @pl.when(pole)
        def _():
            def one(d, carry):
                act(gather_copy(d))
                return carry

            lax.fori_loop(1, n_lon, one, 0)

    each_gather(lambda copy: copy.start())

    def clear(side):
        e[side] = jnp.zeros(e.shape[1:], jnp.float32)

    pl.when(jnp.logical_not(has_north))(lambda: clear(0))
    pl.when(jnp.logical_not(has_south))(lambda: clear(1))

    strips = cols // SUB

    def row_of(t):
        return pl.multiple_of(PAD + t * SUB, SUB)

    def interior(t, carry):
        run(box_strip(x, z1, row_of(t), range(1, last), blocks, lane, {}, {}))
        return carry

    lax.fori_loop(1, strips - 1, interior, 0)

    @pl.when(has_north)
    def _():
        for copy in south_copies:
            copy.wait_recv()

    @pl.when(has_south)
    def _():
        for copy in north_copies:
            copy.wait_recv()

    def merge(t, carry):
        rows = pl.ds(pl.multiple_of(PAD - SUB + t * SUB, SUB), SUB)
        x[inner, rows, :] = jnp.where(lane < LANES // 2, e[1, rows, :], e[0, rows, :])
        return carry

    lax.fori_loop(0, strips + 2, merge, 0)
    each_gather(lambda copy: copy.wait_recv())

    @pl.when(pole)
    def _():
        summed = lax.fori_loop(1, n_lon, lambda d, total: total + gat[d], gat[0])
        k = jnp.where(lat == 0, lane, LANES - 1 - lane)
        third = jnp.where(k < 3, 1.0 / 3.0, 0.0)
        both = third + jnp.where(k < 4, 0.25, 0.0) + jnp.where(k < 5, 0.2, 0.0)
        around = float(cols * n_lon)
        near = jnp.where(k < 5, summed, 0.0)
        means[0] = jnp.full((SUB, LANES), jnp.sum(near * third) / around, jnp.float32)
        means[1] = jnp.full((SUB, LANES), jnp.sum(near * both) / (3.0 * around), jnp.float32)

    @pl.when(jnp.logical_not(pole))
    def _():
        means[...] = jnp.zeros(means.shape, jnp.float32)

    scale, extra = edge_factors(blocks, rows_here, total_rows, lat * rows_here, lane, means[0])

    def sides(t, carry):
        run(box_strip(x, z1, row_of(t), (last, inner, 0), blocks, lane, scale, extra))
        return carry

    lax.fori_loop(1, strips - 1, sides, 0)
    for copy in lon_copies:
        copy.wait_recv()
    whole = list(range(blocks))

    def ends(t, carry):
        strip = t + (t // 2) * (strips - 2)
        row = pl.multiple_of(PAD - SUB + strip * SUB, SUB)
        run(box_strip(x, z1, row, whole, blocks, lane, scale, extra))
        return carry

    lax.fori_loop(0, 4, ends, 0)

    for copy in lon_copies:
        copy.wait_send()

    @pl.when(has_south)
    def _():
        for copy in south_copies:
            copy.wait_send()

    @pl.when(has_north)
    def _():
        for copy in north_copies:
            copy.wait_send()

    each_gather(lambda copy: copy.wait_send())


def second_kernel(n_lat, cols, rows_here, chunk, z1, means, stretch, smooth_hbm, slope_hbm, z2, smooth, slope, sem):
    inner = rows_here // LANES
    blocks = inner + 1
    lat = lax.axis_index("lat")
    lane = lax.broadcasted_iota(jnp.int32, (SUB, LANES), 1)
    scale, extra = edge_factors(
        blocks, rows_here, rows_here * n_lat, lat * rows_here, lane, means[1]
    )
    whole = [inner] + list(range(inner))
    strips = cols // SUB

    def row_of(t):
        return pl.multiple_of(PAD + t * SUB, SUB)

    def smooth_strip(t, keep):
        for b, value in box_strip(z1, z2, row_of(t), whole, blocks, lane, scale, extra):
            if keep and b < inner:
                smooth[pl.ds(pl.multiple_of(t * SUB, SUB), SUB), b * LANES : (b + 1) * LANES] = value

    def slope_strip(t):
        row = row_of(t)

        def rows(b):
            return [z2[b, pl.ds(row + d, SUB), :] for d in (-1, 0, 1)]

        loaded = Strip(blocks, rows)
        across = Strip(blocks, lambda b: loaded[b][2] - loaded[b][0])
        pair = Strip(blocks, lambda b: across[b] + across.ahead(b, 1, lane))
        weighted = Strip(blocks, lambda b: (loaded[b][0] + loaded[b][2]) + (loaded[b][1] + loaded[b][1]))
        for b in range(inner):
            east_west = pair[b] + pair.ahead(b, -1, lane)
            north_south = weighted.ahead(b, 1, lane) - weighted.ahead(b, -1, lane)
            gx = east_west * stretch[pl.ds(b, 1), :]
            gy = north_south * 0.125
            q = 1.0 + gx * gx + gy * gy
            slope[pl.ds(pl.multiple_of(t * SUB, SUB), SUB), b * LANES : (b + 1) * LANES] = q * lax.rsqrt(q)

    smooth_strip(-1, False)
    smooth_strip(0, True)
    smooth_strip(strips, False)
    copies = []
    done = 0
    for c in range(strips // chunk):
        first, end = c * chunk, (c + 1) * chunk

        def both(t, carry):
            smooth_strip(t + 1, True)
            slope_strip(t)
            return carry

        lax.fori_loop(first, min(end, strips - 1), both, 0)
        if end == strips:
            slope_strip(strips - 1)
        rows = pl.ds(first * SUB, chunk * SUB)
        for i, (src, dst) in enumerate(((smooth, smooth_hbm), (slope, slope_hbm))):
            copy = pltpu.make_async_copy(src.at[rows, :], dst.at[0, rows, :], sem.at[i, c])
            copy.start()
            copies.append(copy)
    for copy in copies:
        copy.wait()


def divisor(count, most):
    return max(d for d in range(1, most + 1) if count % d == 0)


def solution(mesh):
    n_lon, n_lat = mesh.shape["lon"], mesh.shape["lat"]

    def local(terrain_relief):
        _, cols, rows_here = terrain_relief.shape
        inner = rows_here // LANES
        blocks = inner + 1
        tall = cols + 2 * PAD
        f32 = jnp.float32
        start = lax.axis_index("lat") * rows_here
        row = (start + jnp.arange(rows_here, dtype=jnp.int32)).astype(f32)
        latitude = jnp.pi * ((row + 0.5) / (rows_here * n_lat) - 0.5)
        stretch = 0.125 / jnp.maximum(jnp.cos(latitude), 0.1)
        stretch = stretch.reshape(inner, LANES)
        vmem = pl.BlockSpec(memory_space=pltpu.VMEM)
        hbm = pl.BlockSpec(memory_space=pltpu.HBM)
        z1, means = pl.pallas_call(
            functools.partial(first_kernel, n_lon, n_lat, cols, rows_here),
            out_shape=(
                jax.ShapeDtypeStruct((blocks, tall, LANES), f32),
                jax.ShapeDtypeStruct((2, SUB, LANES), f32),
            ),
            in_specs=[hbm],
            out_specs=(vmem, vmem),
            scratch_shapes=[
                pltpu.VMEM((blocks, tall, LANES), f32),
                pltpu.VMEM((2, tall, LANES), f32),
                pltpu.VMEM((n_lon, SUB, LANES), f32),
                pltpu.SemaphoreType.DMA((inner,)),
                pltpu.SemaphoreType.DMA((8,)),
                pltpu.SemaphoreType.DMA((8,)),
                pltpu.SemaphoreType.DMA((n_lon,)),
                pltpu.SemaphoreType.DMA((n_lon,)),
            ],
            compiler_params=pltpu.CompilerParams(
                collective_id=0, has_side_effects=True, vmem_limit_bytes=24 * 2**20
            ),
        )(terrain_relief)
        chunk = divisor(cols // SUB, 7)
        return pl.pallas_call(
            functools.partial(second_kernel, n_lat, cols, rows_here, chunk),
            out_shape=(jax.ShapeDtypeStruct(terrain_relief.shape, f32),) * 2,
            in_specs=[vmem, vmem, vmem],
            out_specs=(hbm, hbm),
            scratch_shapes=[
                pltpu.VMEM((blocks, tall, LANES), f32),
                pltpu.VMEM((cols, rows_here), f32),
                pltpu.VMEM((cols, rows_here), f32),
                pltpu.SemaphoreType.DMA((2, cols // SUB // chunk)),
            ],
            compiler_params=pltpu.CompilerParams(vmem_limit_bytes=24 * 2**20),
        )(z1, means, stretch)

    return jax.shard_map(
        local,
        mesh=mesh,
        in_specs=(P(None, "lon", "lat"),),
        out_specs=(P(None, "lon", "lat"), P(None, "lon", "lat")),
        check_vma=False,
    )
```

time: 126 us -> 41.5 us (0.33)
  the two profiles are of different devices: /device:TPU:2 before, /device:TPU:1 now
where the time goes in v1:
time: 41.5 us; the launch traced here: 41.3 us
  Pallas kernels  38.6 us (93%)
  local copies, waits for them, and re-layouts  2.02 us (5%)
  between operations  0.65 us (2%)
    pallas_call x1, Pallas kernels, local(): pl.pallas_call(functools.partial(first_kernel, n_lon, n_lat, cols, rows_h...  21.5 us
    pallas_call x1, Pallas kernels, local(): pl.pallas_call(functools.partial(second_kernel, n_lat, cols, rows_here, c...  17.1 us
    unnamed x2, local copies, waits for them, and re-layouts  2.02 us

profile of v1, /device:TPU:1, one launch (start us, length us, event | category | flops | bytes accessed | tf_op | source)
XLA Modules:
  0.0 41.3 jit_solution(9750781401653364370)
XLA Ops:
  0.6 0.1 maximum_divide_fusion.stretch
  0.7 0.0 copy-start
  0.7 2.0 %copy-done = f32[1,336,2688]{2,1,0:T(8,128)S(1)} copy-done((f32[1,336,2688]{2,1,0:T(8,128)S(1)}, f32[1,336,2688]{2,1,0:T(8,128)}, u32[]{:S(2)}) %copy-start) | copy-done | bytes 3612696
  2.7 21.5 %shard_map.30 = (f32[22,368,128]{2,1,0:T(8,128)S(1)}, f32[2,8,128]{2,1,0:T(8,128)S(1)}) custom-call(f32[1,336,2688]{2,1,0:T(8,128)S(1)} %copy-done), custom_call_target="tpu_custom_call" | custom-call | tf_op jit(solution)/shard_map/pallas_call | solution.py:378
  24.2 17.1 %shard_map.31 = (f32[1,336,2688]{2,1,0:T(8,128)}, f32[1,336,2688]{2,1,0:T(8,128)}) custom-call(f32[22,368,128]{2,1,0:T(8,128)S(1)} %get-tuple-element.4.z1, f32[2,8,128]{2,1,0:T(8,128)S(1)} %get-tuple-element.5.means, f32[21,128]{1,0:T(8,128)S(1)} %maximum_divide_fusion.stretch), custom_call_target="tpu_custom_call" | custom-call | tf_op jit(solution)/shard_map/pallas_call | solution.py:401
Async XLA Ops:
  0.7 2.0 %copy-start = (f32[1,336,2688]{2,1,0:T(8,128)S(1)}, f32[1,336,2688]{2,1,0:T(8,128)}, u32[]{:S(2)}) copy-start(f32[1,336,2688]{2,1,0:T(8,128)} %x_hbm.1) | copy-start | bytes 10838020

commit v2 on v1

--- a/solution.py
+++ b/solution.py
@@ -10,6 +10,8 @@
 LANES = 128
 SUB = 8
 PAD = 16
+HIGH = 16
+MARGIN = 5
 
 
 class Strip:
@@ -37,7 +39,7 @@
 
 def box_strip(src, dst, row, blocks, total_blocks, lane, scale, extra):
     def lon_sum(b):
-        rows = [src[b, pl.ds(row + d, SUB), :] for d in (-2, -1, 0, 1, 2)]
+        rows = [src[b, pl.ds(row + d, HIGH), :] for d in (-2, -1, 0, 1, 2)]
         return ((rows[0] + rows[1]) + (rows[3] + rows[4])) + rows[2]
 
     one = Strip(total_blocks, lon_sum)
@@ -48,7 +50,7 @@
             value = total * scale[b] + extra[b]
         else:
             value = total * (1.0 / 25.0)
-        dst[b, pl.ds(row, SUB), :] = value
+        dst[b, pl.ds(row, HIGH), :] = value
         yield b, value
 
 
@@ -74,8 +76,9 @@
         counted = jnp.maximum(high - low + 1, 1).astype(jnp.float32)
         polar = (row == 0) | (row == total_rows - 1)
         inside = (row > 0) & (row < total_rows - 1)
-        scale[b] = jnp.where(inside, 1.0 / (5.0 * counted), 0.0)
-        extra[b] = jnp.where(polar, mean, 0.0)
+        tiles = HIGH // SUB
+        scale[b] = jnp.concatenate([jnp.where(inside, 1.0 / (5.0 * counted), 0.0)] * tiles, 0)
+        extra[b] = jnp.concatenate([jnp.where(polar, mean, 0.0)] * tiles, 0)
     return scale, extra
 
 
@@ -88,6 +91,7 @@
     has_north, has_south = lat > 0, lat < n_lat - 1
     pole = jnp.logical_not(has_north & has_south)
     lane = lax.broadcasted_iota(jnp.int32, (SUB, LANES), 1)
+    wide = lax.broadcasted_iota(jnp.int32, (HIGH, LANES), 1)
 
     loads = [
         pltpu.make_async_copy(
@@ -137,8 +141,8 @@
         )
 
     own = pl.ds(PAD, cols)
-    head, tail = pl.ds(PAD, SUB), pl.ds(PAD + cols - SUB, SUB)
-    before, after = pl.ds(PAD - SUB, SUB), pl.ds(PAD + cols, SUB)
+    head, tail = pl.ds(PAD, MARGIN), pl.ds(PAD + cols - MARGIN, MARGIN)
+    before, after = pl.ds(PAD - MARGIN, MARGIN), pl.ds(PAD + cols, MARGIN)
     band = pl.ds(0, inner)
     last = inner - 1
     lon_copies = [
@@ -217,13 +221,15 @@
     strips = cols // SUB
 
     def row_of(t):
-        return pl.multiple_of(PAD + t * SUB, SUB)
+        return pl.multiple_of(PAD + SUB + t * HIGH, SUB)
+
+    middle = (cols - 2 * SUB) // HIGH
 
     def interior(t, carry):
-        run(box_strip(x, z1, row_of(t), range(1, last), blocks, lane, {}, {}))
-        return carry
-
-    lax.fori_loop(1, strips - 1, interior, 0)
+        run(box_strip(x, z1, row_of(t), range(1, last), blocks, wide, {}, {}))
+        return carry
+
+    lax.fori_loop(0, middle, interior, 0)
 
     @pl.when(has_north)
     def _():
@@ -261,21 +267,20 @@
     scale, extra = edge_factors(blocks, rows_here, total_rows, lat * rows_here, lane, means[0])
 
     def sides(t, carry):
-        run(box_strip(x, z1, row_of(t), (last, inner, 0), blocks, lane, scale, extra))
-        return carry
-
-    lax.fori_loop(1, strips - 1, sides, 0)
+        run(box_strip(x, z1, row_of(t), (last, inner, 0), blocks, wide, scale, extra))
+        return carry
+
+    lax.fori_loop(0, middle, sides, 0, unroll=2)
     for copy in lon_copies:
         copy.wait_recv()
     whole = list(range(blocks))
 
     def ends(t, carry):
-        strip = t + (t // 2) * (strips - 2)
-        row = pl.multiple_of(PAD - SUB + strip * SUB, SUB)
-        run(box_strip(x, z1, row, whole, blocks, lane, scale, extra))
-        return carry
-
-    lax.fori_loop(0, 4, ends, 0)
+        row = pl.multiple_of(PAD - SUB + t * cols, SUB)
+        run(box_strip(x, z1, row, whole, blocks, wide, scale, extra))
+        return carry
+
+    lax.fori_loop(0, 2, ends, 0)
 
     for copy in lon_copies:
         copy.wait_send()
@@ -298,61 +303,66 @@
     blocks = inner + 1
     lat = lax.axis_index("lat")
     lane = lax.broadcasted_iota(jnp.int32, (SUB, LANES), 1)
+    wide = lax.broadcasted_iota(jnp.int32, (HIGH, LANES), 1)
     scale, extra = edge_factors(
         blocks, rows_here, rows_here * n_lat, lat * rows_here, lane, means[1]
     )
     whole = [inner] + list(range(inner))
-    strips = cols // SUB
-
-    def row_of(t):
-        return pl.multiple_of(PAD + t * SUB, SUB)
-
-    def smooth_strip(t, keep):
-        for b, value in box_strip(z1, z2, row_of(t), whole, blocks, lane, scale, extra):
-            if keep and b < inner:
-                smooth[pl.ds(pl.multiple_of(t * SUB, SUB), SUB), b * LANES : (b + 1) * LANES] = value
-
-    def slope_strip(t):
-        row = row_of(t)
-
+    strips = cols // HIGH
+
+    def smooth_strip(row, out_row):
+        for b, value in box_strip(z1, z2, row, whole, blocks, wide, scale, extra):
+            if b < inner:
+                smooth[pl.ds(out_row, HIGH), b * LANES : (b + 1) * LANES] = value
+
+    def slope_strip(row, out_row):
         def rows(b):
-            return [z2[b, pl.ds(row + d, SUB), :] for d in (-1, 0, 1)]
+            return [z2[b, pl.ds(row + d, HIGH), :] for d in (-1, 0, 1)]
 
         loaded = Strip(blocks, rows)
         across = Strip(blocks, lambda b: loaded[b][2] - loaded[b][0])
-        pair = Strip(blocks, lambda b: across[b] + across.ahead(b, 1, lane))
+        pair = Strip(blocks, lambda b: across[b] + across.ahead(b, 1, wide))
         weighted = Strip(blocks, lambda b: (loaded[b][0] + loaded[b][2]) + (loaded[b][1] + loaded[b][1]))
         for b in range(inner):
-            east_west = pair[b] + pair.ahead(b, -1, lane)
-            north_south = weighted.ahead(b, 1, lane) - weighted.ahead(b, -1, lane)
+            east_west = pair[b] + pair.ahead(b, -1, wide)
+            north_south = weighted.ahead(b, 1, wide) - weighted.ahead(b, -1, wide)
             gx = east_west * stretch[pl.ds(b, 1), :]
             gy = north_south * 0.125
             q = 1.0 + gx * gx + gy * gy
-            slope[pl.ds(pl.multiple_of(t * SUB, SUB), SUB), b * LANES : (b + 1) * LANES] = q * lax.rsqrt(q)
-
-    smooth_strip(-1, False)
-    smooth_strip(0, True)
-    smooth_strip(strips, False)
-    copies = []
-    done = 0
-    for c in range(strips // chunk):
-        first, end = c * chunk, (c + 1) * chunk
-
-        def both(t, carry):
-            smooth_strip(t + 1, True)
-            slope_strip(t)
-            return carry
-
-        lax.fori_loop(first, min(end, strips - 1), both, 0)
-        if end == strips:
-            slope_strip(strips - 1)
-        rows = pl.ds(first * SUB, chunk * SUB)
-        for i, (src, dst) in enumerate(((smooth, smooth_hbm), (slope, slope_hbm))):
-            copy = pltpu.make_async_copy(src.at[rows, :], dst.at[0, rows, :], sem.at[i, c])
-            copy.start()
-            copies.append(copy)
-    for copy in copies:
-        copy.wait()
+            slope[pl.ds(out_row, HIGH), b * LANES : (b + 1) * LANES] = q * lax.rsqrt(q)
+
+    def copies(c):
+        start = pl.multiple_of(c * (chunk * HIGH), SUB)
+        rows = pl.ds(start, chunk * HIGH)
+        return [
+            pltpu.make_async_copy(
+                src.at[pl.ds(start + lead, chunk * HIGH), :], dst.at[0, rows, :], sem.at[i, c]
+            )
+            for i, (src, dst, lead) in enumerate(
+                ((smooth, smooth_hbm, SUB), (slope, slope_hbm, 2 * HIGH))
+            )
+        ]
+
+    def step(u, carry):
+        out_row = pl.multiple_of(u * HIGH, SUB)
+        slope_strip(pl.multiple_of(PAD + jnp.maximum(u - 2, 0) * HIGH, SUB), out_row)
+        smooth_strip(pl.multiple_of(PAD - SUB + jnp.minimum(u, strips) * HIGH, SUB), out_row)
+
+        @pl.when((u > 2) & (lax.rem(u + chunk - 1, chunk) == 0))
+        def _():
+            for copy in copies(jnp.maximum(u - 1, chunk) // chunk - 1):
+                copy.start()
+
+        return carry
+
+    lax.fori_loop(0, strips + 2, step, 0)
+
+    def finish(c, carry):
+        for copy in copies(c):
+            copy.wait()
+        return carry
+
+    lax.fori_loop(0, strips // chunk, finish, 0)
 
 
 def divisor(count, most):
@@ -378,8 +388,8 @@
         z1, means = pl.pallas_call(
             functools.partial(first_kernel, n_lon, n_lat, cols, rows_here),
             out_shape=(
-                jax.ShapeDtypeStruct((blocks, tall, LANES), f32),
-                jax.ShapeDtypeStruct((2, SUB, LANES), f32),
+                pltpu.VMEM((blocks, tall, LANES), f32),
+                pltpu.VMEM((2, SUB, LANES), f32),
             ),
             in_specs=[hbm],
             out_specs=(vmem, vmem),
@@ -394,10 +404,10 @@
                 pltpu.SemaphoreType.DMA((n_lon,)),
             ],
             compiler_params=pltpu.CompilerParams(
-                collective_id=0, has_side_effects=True, vmem_limit_bytes=24 * 2**20
+                collective_id=0, has_side_effects=True, vmem_limit_bytes=54 * 2**20
             ),
         )(terrain_relief)
-        chunk = divisor(cols // SUB, 7)
+        chunk = divisor(cols // HIGH, 4)
         return pl.pallas_call(
             functools.partial(second_kernel, n_lat, cols, rows_here, chunk),
             out_shape=(jax.ShapeDtypeStruct(terrain_relief.shape, f32),) * 2,
@@ -405,9 +415,9 @@
             out_specs=(hbm, hbm),
             scratch_shapes=[
                 pltpu.VMEM((blocks, tall, LANES), f32),
-                pltpu.VMEM((cols, rows_here), f32),
-                pltpu.VMEM((cols, rows_here), f32),
-                pltpu.SemaphoreType.DMA((2, cols // SUB // chunk)),
+                pltpu.VMEM((tall, rows_here), f32),
+                pltpu.VMEM((tall, rows_here), f32),
+                pltpu.SemaphoreType.DMA((2, cols // HIGH // chunk)),
             ],
             compiler_params=pltpu.CompilerParams(vmem_limit_bytes=24 * 2**20),
         )(z1, means, stretch)

time: 41.5 us -> 62.2 us (1.50)
  Pallas kernels: 38.6 us -> 61.3 us
  local copies, waits for them, and re-layouts: 2.02 us -> 0 us
    pallas_call x1, Pallas kernels: 17.1 us -> 46.2 us  [local(): pl.pallas_call(functools.partial(second_kernel, n_lat, cols, rows_here, c...]
    pallas_call x1, Pallas kernels: 21.5 us -> 15.1 us  [local(): pl.pallas_call(functools.partial(first_kernel, n_lon, n_lat, cols, rows_h...]
    unnamed x2 -> x0, local copies, waits for them, and re-layouts: 2.02 us -> none
where the time goes in v2:
time: 62.2 us; the launch traced here: 62 us
  Pallas kernels  61.3 us (99%)
  between operations  0.64 us (1%)
    pallas_call x1, Pallas kernels, local(): pl.pallas_call(functools.partial(second_kernel, n_lat, cols, rows_here, c...  46.2 us
    pallas_call x1, Pallas kernels, local(): pl.pallas_call(functools.partial(first_kernel, n_lon, n_lat, cols, rows_h...  15.1 us

profile of v2, /device:TPU:1, one launch (start us, length us, event | category | flops | bytes accessed | tf_op | source)
XLA Modules:
  0.0 62.0 jit_solution(5963689490815954279)
XLA Ops:
  0.6 0.1 maximum_divide_fusion.stretch
  0.7 15.1 %shard_map.30 = (f32[22,368,128]{2,1,0:T(8,128)S(1)}, f32[2,8,128]{2,1,0:T(8,128)S(1)}) custom-call(f32[1,336,2688]{2,1,0:T(8,128)} %x_hbm.1), custom_call_target="tpu_custom_call" | custom-call | tf_op jit(solution)/shard_map/pallas_call | solution.py:388
  15.8 46.2 %shard_map.31 = (f32[1,336,2688]{2,1,0:T(8,128)}, f32[1,336,2688]{2,1,0:T(8,128)}) custom-call(f32[22,368,128]{2,1,0:T(8,128)S(1)} %get-tuple-element.4.z1, f32[2,8,128]{2,1,0:T(8,128)S(1)} %get-tuple-element.5.means, f32[21,128]{1,0:T(8,128)S(1)} %maximum_divide_fusion.stretch), custom_call_target="tpu_custom_call" | custom-call | tf_op jit(solution)/shard_map/pallas_call | solution.py:411

commit v3 on v2

--- a/solution.py
+++ b/solution.py
@@ -11,6 +11,7 @@
 SUB = 8
 PAD = 16
 HIGH = 16
+STEP = 8
 MARGIN = 5
 
 
@@ -38,8 +39,10 @@
 
 
 def box_strip(src, dst, row, blocks, total_blocks, lane, scale, extra):
+    high = lane.shape[0]
+
     def lon_sum(b):
-        rows = [src[b, pl.ds(row + d, HIGH), :] for d in (-2, -1, 0, 1, 2)]
+        rows = [src[b, pl.ds(row + d, high), :] for d in (-2, -1, 0, 1, 2)]
         return ((rows[0] + rows[1]) + (rows[3] + rows[4])) + rows[2]
 
     one = Strip(total_blocks, lon_sum)
@@ -50,7 +53,7 @@
             value = total * scale[b] + extra[b]
         else:
             value = total * (1.0 / 25.0)
-        dst[b, pl.ds(row, HIGH), :] = value
+        dst[b, pl.ds(row, high), :] = value
         yield b, value
 
 
@@ -68,7 +71,7 @@
     }
 
 
-def edge_factors(blocks, rows_here, total_rows, start, lane, mean):
+def edge_factors(blocks, rows_here, total_rows, start, lane, mean, step):
     scale, extra = {}, {}
     for b, row in edge_rows(blocks, rows_here, start, lane).items():
         low = jnp.maximum(row - 2, 0)
@@ -76,7 +79,7 @@
         counted = jnp.maximum(high - low + 1, 1).astype(jnp.float32)
         polar = (row == 0) | (row == total_rows - 1)
         inside = (row > 0) & (row < total_rows - 1)
-        tiles = HIGH // SUB
+        tiles = step // SUB
         scale[b] = jnp.concatenate([jnp.where(inside, 1.0 / (5.0 * counted), 0.0)] * tiles, 0)
         extra[b] = jnp.concatenate([jnp.where(polar, mean, 0.0)] * tiles, 0)
     return scale, extra
@@ -264,7 +267,7 @@
     def _():
         means[...] = jnp.zeros(means.shape, jnp.float32)
 
-    scale, extra = edge_factors(blocks, rows_here, total_rows, lat * rows_here, lane, means[0])
+    scale, extra = edge_factors(blocks, rows_here, total_rows, lat * rows_here, lane, means[0], HIGH)
 
     def sides(t, carry):
         run(box_strip(x, z1, row_of(t), (last, inner, 0), blocks, wide, scale, extra))
@@ -303,21 +306,22 @@
     blocks = inner + 1
     lat = lax.axis_index("lat")
     lane = lax.broadcasted_iota(jnp.int32, (SUB, LANES), 1)
-    wide = lax.broadcasted_iota(jnp.int32, (HIGH, LANES), 1)
+    wide = lax.broadcasted_iota(jnp.int32, (STEP, LANES), 1)
     scale, extra = edge_factors(
-        blocks, rows_here, rows_here * n_lat, lat * rows_here, lane, means[1]
+        blocks, rows_here, rows_here * n_lat, lat * rows_here, lane, means[1], STEP
     )
     whole = [inner] + list(range(inner))
-    strips = cols // HIGH
+    lag = (STEP + 2 * SUB + STEP - 1) // STEP
+    strips = (cols + 2 * SUB) // STEP
 
     def smooth_strip(row, out_row):
         for b, value in box_strip(z1, z2, row, whole, blocks, wide, scale, extra):
             if b < inner:
-                smooth[pl.ds(out_row, HIGH), b * LANES : (b + 1) * LANES] = value
+                smooth[pl.ds(out_row, STEP), b * LANES : (b + 1) * LANES] = value
 
     def slope_strip(row, out_row):
         def rows(b):
-            return [z2[b, pl.ds(row + d, HIGH), :] for d in (-1, 0, 1)]
+            return [z2[b, pl.ds(row + d, STEP), :] for d in (-1, 0, 1)]
 
         loaded = Strip(blocks, rows)
         across = Strip(blocks, lambda b: loaded[b][2] - loaded[b][0])
@@ -329,40 +333,40 @@
             gx = east_west * stretch[pl.ds(b, 1), :]
             gy = north_south * 0.125
             q = 1.0 + gx * gx + gy * gy
-            slope[pl.ds(out_row, HIGH), b * LANES : (b + 1) * LANES] = q * lax.rsqrt(q)
+            slope[pl.ds(out_row, STEP), b * LANES : (b + 1) * LANES] = q * lax.rsqrt(q)
 
     def copies(c):
-        start = pl.multiple_of(c * (chunk * HIGH), SUB)
-        rows = pl.ds(start, chunk * HIGH)
+        start = pl.multiple_of(c * (chunk * STEP), SUB)
+        rows = pl.ds(start, chunk * STEP)
         return [
             pltpu.make_async_copy(
-                src.at[pl.ds(start + lead, chunk * HIGH), :], dst.at[0, rows, :], sem.at[i, c]
+                src.at[pl.ds(start + lead, chunk * STEP), :], dst.at[0, rows, :], sem.at[i, c]
             )
             for i, (src, dst, lead) in enumerate(
-                ((smooth, smooth_hbm, SUB), (slope, slope_hbm, 2 * HIGH))
+                ((smooth, smooth_hbm, SUB), (slope, slope_hbm, lag * STEP))
             )
         ]
 
     def step(u, carry):
-        out_row = pl.multiple_of(u * HIGH, SUB)
-        slope_strip(pl.multiple_of(PAD + jnp.maximum(u - 2, 0) * HIGH, SUB), out_row)
-        smooth_strip(pl.multiple_of(PAD - SUB + jnp.minimum(u, strips) * HIGH, SUB), out_row)
-
-        @pl.when((u > 2) & (lax.rem(u + chunk - 1, chunk) == 0))
+        out_row = pl.multiple_of(u * STEP, SUB)
+        slope_strip(pl.multiple_of(PAD + jnp.maximum(u - lag, 0) * STEP, SUB), out_row)
+        smooth_strip(pl.multiple_of(PAD - SUB + jnp.minimum(u, strips - 1) * STEP, SUB), out_row)
+
+        @pl.when((u >= lag) & (lax.rem(u + 1 + chunk * lag - lag, chunk) == 0))
         def _():
-            for copy in copies(jnp.maximum(u - 1, chunk) // chunk - 1):
+            for copy in copies(jnp.maximum(u + 1 - lag, chunk) // chunk - 1):
                 copy.start()
 
         return carry
 
-    lax.fori_loop(0, strips + 2, step, 0)
+    lax.fori_loop(0, cols // STEP + lag, step, 0)
 
     def finish(c, carry):
         for copy in copies(c):
             copy.wait()
         return carry
 
-    lax.fori_loop(0, strips // chunk, finish, 0)
+    lax.fori_loop(0, cols // STEP // chunk, finish, 0)
 
 
 def divisor(count, most):
@@ -407,7 +411,7 @@
                 collective_id=0, has_side_effects=True, vmem_limit_bytes=54 * 2**20
             ),
         )(terrain_relief)
-        chunk = divisor(cols // HIGH, 4)
+        chunk = divisor(cols // STEP, 64 // STEP)
         return pl.pallas_call(
             functools.partial(second_kernel, n_lat, cols, rows_here, chunk),
             out_shape=(jax.ShapeDtypeStruct(terrain_relief.shape, f32),) * 2,
@@ -417,7 +421,7 @@
                 pltpu.VMEM((blocks, tall, LANES), f32),
                 pltpu.VMEM((tall, rows_here), f32),
                 pltpu.VMEM((tall, rows_here), f32),
-                pltpu.SemaphoreType.DMA((2, cols // HIGH // chunk)),
+                pltpu.SemaphoreType.DMA((2, cols // STEP // chunk)),
             ],
             compiler_params=pltpu.CompilerParams(vmem_limit_bytes=24 * 2**20),
         )(z1, means, stretch)

time: 62.2 us -> 32.7 us (0.53)
  Pallas kernels: 61.3 us -> 31.8 us
    pallas_call x1, Pallas kernels: 46.2 us -> 16.8 us  [local(): pl.pallas_call(functools.partial(second_kernel, n_lat, cols, rows_here, c...]
where the time goes in v3:
time: 32.7 us; the launch traced here: 32.6 us
  Pallas kernels  31.8 us (97%)
  between operations  0.64 us (2%)
    pallas_call x1, Pallas kernels, local(): pl.pallas_call(functools.partial(second_kernel, n_lat, cols, rows_here, c...  16.8 us
    pallas_call x1, Pallas kernels, local(): pl.pallas_call(functools.partial(first_kernel, n_lon, n_lat, cols, rows_h...  15.1 us

profile of v3, /device:TPU:1, one launch (start us, length us, event | category | flops | bytes accessed | tf_op | source)
XLA Modules:
  0.0 32.6 jit_solution(7023098764555979443)
XLA Ops:
  0.6 0.1 maximum_divide_fusion.stretch
  0.7 15.1 %shard_map.30 = (f32[22,368,128]{2,1,0:T(8,128)S(1)}, f32[2,8,128]{2,1,0:T(8,128)S(1)}) custom-call(f32[1,336,2688]{2,1,0:T(8,128)} %x_hbm.1), custom_call_target="tpu_custom_call" | custom-call | tf_op jit(solution)/shard_map/pallas_call | solution.py:392
  15.8 16.8 %shard_map.31 = (f32[1,336,2688]{2,1,0:T(8,128)}, f32[1,336,2688]{2,1,0:T(8,128)}) custom-call(f32[22,368,128]{2,1,0:T(8,128)S(1)} %get-tuple-element.4.z1, f32[2,8,128]{2,1,0:T(8,128)S(1)} %get-tuple-element.5.means, f32[21,128]{1,0:T(8,128)S(1)} %maximum_divide_fusion.stretch), custom_call_target="tpu_custom_call" | custom-call | tf_op jit(solution)/shard_map/pallas_call | solution.py:415

commit v4 on v3

--- a/solution.py
+++ b/solution.py
@@ -49,6 +49,34 @@
     two = Strip(total_blocks, lambda b: one[b] + one.ahead(b, 1, lane))
     for b in blocks:
         total = (two[b] + two.ahead(b, -2, lane)) + one.ahead(b, 2, lane)
+        if b in scale:
+            value = total * scale[b] + extra[b]
+        else:
+            value = total * (1.0 / 25.0)
+        dst[b, pl.ds(row, high), :] = value
+        yield b, value
+
+
+def banded_strip(src, dst, row, high, total_blocks, band, scale, extra):
+    def parts(b):
+        rows = [src[b, pl.ds(row + d, high), :] for d in (-2, -1, 0, 1, 2)]
+        total = ((rows[0] + rows[1]) + (rows[3] + rows[4])) + rows[2]
+        large = total.astype(jnp.bfloat16).astype(jnp.float32)
+        return jnp.concatenate([large, total - large], 0).astype(jnp.bfloat16)
+
+    split = [parts(b) for b in range(total_blocks)]
+    left = jnp.concatenate(
+        [
+            jnp.concatenate([split[(b + d) % total_blocks] for d in (-1, 0, 1, 2)], 1)
+            for b in range(0, total_blocks, 2)
+        ],
+        0,
+    )
+    sums = jnp.dot(left, band[...], preferred_element_type=jnp.float32)
+    for b in range(total_blocks):
+        lanes = slice(b % 2 * LANES, (b % 2 + 1) * LANES)
+        first = b // 2 * 2 * high
+        total = sums[first : first + high, lanes] + sums[first + high : first + 2 * high, lanes]
         if b in scale:
             value = total * scale[b] + extra[b]
         else:
@@ -301,7 +329,7 @@
     each_gather(lambda copy: copy.wait_send())
 
 
-def second_kernel(n_lat, cols, rows_here, chunk, z1, means, stretch, smooth_hbm, slope_hbm, z2, smooth, slope, sem):
+def second_kernel(n_lat, cols, rows_here, chunk, z1, means, stretch, band, smooth_hbm, slope_hbm, z2, smooth, slope, sem):
     inner = rows_here // LANES
     blocks = inner + 1
     lat = lax.axis_index("lat")
@@ -310,12 +338,11 @@
     scale, extra = edge_factors(
         blocks, rows_here, rows_here * n_lat, lat * rows_here, lane, means[1], STEP
     )
-    whole = [inner] + list(range(inner))
     lag = (STEP + 2 * SUB + STEP - 1) // STEP
     strips = (cols + 2 * SUB) // STEP
 
     def smooth_strip(row, out_row):
-        for b, value in box_strip(z1, z2, row, whole, blocks, wide, scale, extra):
+        for b, value in banded_strip(z1, z2, row, STEP, blocks, band, scale, extra):
             if b < inner:
                 smooth[pl.ds(out_row, STEP), b * LANES : (b + 1) * LANES] = value
 
@@ -387,6 +414,8 @@
         latitude = jnp.pi * ((row + 0.5) / (rows_here * n_lat) - 0.5)
         stretch = 0.125 / jnp.maximum(jnp.cos(latitude), 0.1)
         stretch = stretch.reshape(inner, LANES)
+        offset = jnp.arange(4 * LANES)[:, None] - LANES - jnp.arange(2 * LANES)[None, :]
+        band = (jnp.abs(offset) <= 2).astype(jnp.bfloat16)
         vmem = pl.BlockSpec(memory_space=pltpu.VMEM)
         hbm = pl.BlockSpec(memory_space=pltpu.HBM)
         z1, means = pl.pallas_call(
@@ -415,7 +444,7 @@
         return pl.pallas_call(
             functools.partial(second_kernel, n_lat, cols, rows_here, chunk),
             out_shape=(jax.ShapeDtypeStruct(terrain_relief.shape, f32),) * 2,
-            in_specs=[vmem, vmem, vmem],
+            in_specs=[vmem, vmem, vmem, vmem],
             out_specs=(hbm, hbm),
             scratch_shapes=[
                 pltpu.VMEM((blocks, tall, LANES), f32),
@@ -424,7 +453,7 @@
                 pltpu.SemaphoreType.DMA((2, cols // STEP // chunk)),
             ],
             compiler_params=pltpu.CompilerParams(vmem_limit_bytes=24 * 2**20),
-        )(z1, means, stretch)
+        )(z1, means, stretch, band)
 
     return jax.shard_map(
         local,

time: 32.7 us -> 28.3 us (0.87)
  Pallas kernels: 31.8 us -> 27.2 us
    pallas_call x1, Pallas kernels: 16.8 us -> 12.2 us  [local(): pl.pallas_call(functools.partial(second_kernel, n_lat, cols, rows_here, c...]
where the time goes in v4:
time: 28.3 us; the launch traced here: 28.1 us
  Pallas kernels  27.2 us (96%)
  between operations  0.66 us (2%)
    pallas_call x1, Pallas kernels, local(): pl.pallas_call(functools.partial(first_kernel, n_lon, n_lat, cols, rows_h...  15.1 us
    pallas_call x1, Pallas kernels, local(): pl.pallas_call(functools.partial(second_kernel, n_lat, cols, rows_here, c...  12.2 us

profile of v4, /device:TPU:1, one launch (start us, length us, event | category | flops | bytes accessed | tf_op | source)
XLA Modules:
  0.0 28.1 jit_solution(8369147156024173897)
XLA Ops:
  0.6 0.1 maximum_divide_fusion.stretch
  0.7 0.2 fusion.band
  0.9 15.1 %shard_map.30 = (f32[22,368,128]{2,1,0:T(8,128)S(1)}, f32[2,8,128]{2,1,0:T(8,128)S(1)}) custom-call(f32[1,336,2688]{2,1,0:T(8,128)} %x_hbm.1), custom_call_target="tpu_custom_call" | custom-call | tf_op jit(solution)/shard_map/pallas_call | solution.py:421
  16.0 12.2 %shard_map.31 = (f32[1,336,2688]{2,1,0:T(8,128)}, f32[1,336,2688]{2,1,0:T(8,128)}) custom-call(f32[22,368,128]{2,1,0:T(8,128)S(1)} %get-tuple-element.4.z1, f32[2,8,128]{2,1,0:T(8,128)S(1)} %get-tuple-element.5.means, f32[21,128]{1,0:T(8,128)S(1)} %maximum_divide_fusion.stretch, bf16[512,256]{1,0:T(8,128)(2,1)S(1)} %fusion.band), custom_call_target="tpu_custom_call" | custom-call | tf_op jit(solution)/shard_map/pallas_call | solution.py:444
  (1 shorter events, 0.0 us)
